TPU v7x, 32 devices: a whole 2x2x4 slice. The times are simulated.
32 devices in a mesh: wl: 8 (over y, x, core), tile: 4 (over z).
Axes of the slice: x: 2, y: 2, z: 4, core: 2. Of those that a mesh axis runs over, the one named last changes fastest.
Arguments:
- forward: float32 [32, 2, 1024, 1024], P(('wl', 'tile')), may hold values from -6 to 6
- adjoint: float32 [32, 2, 1024, 1024], P(('wl', 'tile')), may hold values from -6 to 6
- mode: float32 [2, 1024], replicated, may hold values from -6 to 6
- target: float32 [32], P(('wl', 'tile')), may hold values from 0 to 2
- wl_index: int32 [32], P(('wl', 'tile')), may hold values from 0 to 31, each once
- tile_of: int32 [32], replicated, may hold values from 0 to 31, each once
- density: float32 [1024, 1024], P(('wl', 'tile')), may hold values from 0 to 1
Outputs:
- gradient: float32 [1024, 1024], P(('wl', 'tile'))
All inputs are finite; a program needn't handle non-finite values.
Results may differ from a plain program's by a relative error of at most 0.00002.
Values sent between devices are 32-bit elements; how exact they have to be, the bound alone decides.
A program may use at most 64 MiB of HBM per device.

v0:
```python
import jax
import jax.numpy as jnp
from jax import lax
from jax.sharding import PartitionSpec as P


def per_device(forward, adjoint, mode, target, wl_index, tile_of, density):
    wide = lax.axis_size("wl")
    narrow = lax.axis_size("tile")
    devices = wide * narrow
    rows = forward.shape[2]
    cols = forward.shape[3]
    fwd_re, fwd_im = (forward[0, 0], forward[0, 1])
    adj_re, adj_im = (adjoint[0, 0], adjoint[0, 1])
    mon = rows // 2
    over_re = jnp.sum(fwd_re[mon] * mode[0] - fwd_im[mon] * mode[1])
    over_im = jnp.sum(fwd_re[mon] * mode[1] + fwd_im[mon] * mode[0])
    fom = (over_re * over_re + over_im * over_im) / cols
    freq = 1.0 + wl_index[0].astype(jnp.float32) / devices
    field = freq * freq * (fwd_re * adj_re - fwd_im * adj_im)
    tile_rows = rows // devices
    order = tile_of.reshape(wide, narrow).T.reshape(devices)
    total_fom = lax.psum(fom, ("wl", "tile"))
    scale = total_fom / devices + 1.0
    weight = target[0] - fom / scale
    partial_tiles = lax.psum_scatter(
        (weight * field).reshape(devices, tile_rows, cols)[order].reshape(rows, cols),
        "tile",
        scatter_dimension=0,
        tiled=True,
    )
    owned = lax.psum_scatter(partial_tiles, "wl", scatter_dimension=0, tiled=True)
    slope = 4.0 * (1.0 - jnp.tanh(4.0 * (density - 0.5)) ** 2)
    shaped = owned * slope
    squares = lax.psum(jnp.sum(shaped * shaped), ("wl", "tile"))
    return shaped / jnp.sqrt(squares / (rows * cols) + 1e-06)


def solution(mesh):
    in_specs = (
        P(("wl", "tile"), None, None, None),
        P(("wl", "tile"), None, None, None),
        P(),
        P(("wl", "tile")),
        P(("wl", "tile")),
        P(),
        P(("wl", "tile"), None),
    )
    out_specs = P(("wl", "tile"), None)
    return jax.shard_map(
        per_device, mesh=mesh, in_specs=in_specs, out_specs=out_specs, check_vma=False
    )
```

profile of v0, /device:TPU:0, one launch (start us, length us, event | category | flops | bytes accessed | tf_op | source)
XLA Modules:
  0.0 236.6 jit_solution(16246562870266419326)
XLA Ops:
  6.5 0.0 reduce-scatter.3.cloned.1.call-start
  7.2 0.7 reshape.59
  7.9 0.1 copy.9
  8.0 0.1 reshape.60
  8.1 0.8 fusion.2
  8.9 0.8 fusion.1
  9.7 0.7 add_reduce_fusion
  13.5 42.0 %psum.14 = f32[]{:T(128)} all-reduce(f32[]{:T(128)S(6)} %div.21), channel_id=1, replica_groups=mesh['wl'=8,'tile'=4] {'wl','tile'}, use_global_device_ids=true, to_apply=%region_2.0 | all-reduce | flops 1 | bytes 8 | tf_op jit(solution)/shard_map/psum | solution.py:23
  56.1 8.8 %multiply_multiply_fusion = f32[1,1,1024,1024]{3,2,1,0:T(8,128)} fusion(f32[1,2,1024,1024]{3,2,1,0:T(8,128)} %param.8, f32[1,2,1024,1024]{3,2,1,0:T(8,128)} %param.7, f32[]{:T(128)} %bitcast.5, f32[]{:T(128)S(6)} %sub.22), kind=kLoop, calls=%fused_computation.1 | loop fusion | flops 5242880 | bytes 20971528 | tf_op jit(solution)/shard_map/mul | solution.py:27
  64.9 4.9 %gather_fusion = f32[32,32,1024]{2,1,0:T(8,128)} fusion(f32[32,32,1024]{2,1,0:T(8,128)} %bitcast.13, s32[1024]{0:T(1024)S(1)} %pad_clamp_fusion), kind=kCustom, calls=%fused_computation | custom fusion | bytes 8388736 | tf_op jit(solution)/shard_map/gather | solution.py:27
  69.8 0.0 copy-start
  69.8 0.0 reduce-scatter.3.cloned.1.call-update
  69.9 0.0 reduce-scatter.5.cloned.1.call-start
  69.9 76.9 %reduce-scatter.3.cloned.1.call-done = f32[256,1024]{1,0:T(8,128)} async-done(((f32[1024,1024]{1,0:T(8,128)}), f32[256,1024]{1,0:T(8,128)}) %reduce-scatter.3.cloned.1.call-update) | async-done | bytes 1048592 | tf_op jit(solution)/shard_map/reduce_scatter | solution.py:26
  146.8 0.0 reduce-scatter.5.cloned.1.call-update
  146.8 39.6 %reduce-scatter.5.cloned.1.call-done = f32[32,1024]{1,0:T(8,128)} async-done(((f32[256,1024]{1,0:T(8,128)}), f32[32,1024]{1,0:T(8,128)}) %reduce-scatter.5.cloned.1.call-update) | async-done | bytes 131088 | tf_op jit(solution)/shard_map/reduce_scatter | solution.py:32
  186.5 0.0 copy-done
  186.5 1.6 multiply_reduce_fusion
  188.0 39.5 %psum.15 = f32[]{:T(128)} all-reduce(f32[]{:T(128)} %multiply_reduce_fusion), channel_id=1, replica_groups=mesh['wl'=8,'tile'=4] {'wl','tile'}, use_global_device_ids=true, to_apply=%region_6.0 | all-reduce | flops 1 | bytes 8 | tf_op jit(solution)/shard_map/psum | solution.py:35
  228.2 1.6 broadcast_divide_fusion
  (2 shorter events, 0.0 us)
Async XLA Ops:
  6.5 140.3 %reduce-scatter.3.cloned.1.call-start = ((), (), s32[]{:S(2)}) async-start(), calls=%async_computation.2 | async-start | bytes 5242880 | tf_op jit(solution)/shard_map/reduce_scatter | solution.py:26
  69.8 116.6 %copy-start = (f32[32,1024]{1,0:T(8,128)S(1)}, f32[32,1024]{1,0:T(8,128)}, u32[]{:S(2)}) copy-start(f32[32,1024]{1,0:T(8,128)} %param.13) | copy-start | bytes 393220
  69.9 116.6 %reduce-scatter.5.cloned.1.call-start = ((), (), s32[]{:S(2)}) async-start(), calls=%async_computation.3 | async-start | bytes 1179648 | tf_op jit(solution)/shard_map/reduce_scatter | solution.py:32
Sparse Core Ops, SparseCore 0:
  70.0 76.7 reduce-scatter.2
  150.0 36.4 reduce-scatter.4
where the time goes:
time: 237 us
  waiting for transfers between devices  117 us (49%)
  blocking collectives  81.5 us (34%)
  between operations  18.5 us (8%)
  other arithmetic  12.7 us (5%)
  local copies, waits for them, and re-layouts  7.4 us (3%)
    reduce_scatter x1, waiting for transfers between devices, per_device(): lax.psum_scatter((weight * field).reshape(devices, tile_rows, cols)[order...  76.9 us
    psum x1, blocking collectives, per_device(): total_fom = lax.psum(fom, ('wl', 'tile'))  42 us
    reduce_scatter x1, waiting for transfers between devices, per_device(): lax.psum_scatter(partial_tiles, 'wl', scatter_dimension=0, tiled=True)  39.6 us
    psum x1, blocking collectives, per_device(): squares = lax.psum(jnp.sum(shaped * shaped), ('wl', 'tile'))  39.5 us
    mul x1, other arithmetic, per_device(): weight * field  8.8 us
    gather x1, local copies, waits for them, and re-layouts, per_device(): (weight * field).reshape(devices, tile_rows, cols)[order]  4.93 us
  transfers between devices with their start and end apart: 2, of which 2 were waited for; matrix products, arithmetic and copies ran while one was open for 0% of the time, Pallas kernels for 0%

commit v1 on v0

v1 whole, which is shorter than its diff:
```python
import functools

import jax
import jax.numpy as jnp
from jax import lax
from jax.experimental import pallas as pl
from jax.experimental.pallas import tpu as pltpu
from jax.sharding import PartitionSpec as P

MESH = pl.DeviceIdType.MESH
SUB = 8
LANES = 128
PIECES = 8


def plane(wide):
    cores = 2 if wide % 2 == 0 else 1
    chips = wide // cores
    first = max(f for f in range(1, chips + 1) if chips % f == 0 and f * f <= chips)
    return first, chips // first, cores


def kernel(
    sizes, tile_of, target, wl_index, mode, density, fwd, adj, shaped_out, squares_out,
    line, f_src, f_recv, q_src, q_recv, slope, own, away, r0, r1, r2, r3,
    in_sem, f_ssem, f_rsem, q_ssem, q_rsem, s0, e0, s1, e1, s2, e2, s3, e3, *bufs,
):
    g1, g2, cores, deep, groups, parts, rows, cols = sizes
    wide = g1 * g2 * cores
    devices = wide * deep
    tile_rows = rows // devices
    per_core = g1 * g2 * deep
    width = cols // parts
    f_bufs, a_bufs = bufs[:groups], bufs[groups:]
    w_me, z_me = lax.axis_index("wl"), lax.axis_index("tile")
    me = w_me * deep + z_me
    c_me = w_me % cores
    b_me = (w_me // cores) % g2
    a_me = w_me // (cores * g2)

    def at(a, b, c, z):
        return ((a * g2 + b) * cores + c, z)

    def everyone(o):
        f = (me + o) % devices
        return (f // deep, f % deep)

    mon = rows // 2
    mt, mk, ms = mon // tile_rows, (mon % tile_rows) // SUB, mon % SUB
    line_copy = pltpu.make_async_copy(fwd.at[:, mt, mk], line, in_sem.at[2 * groups])
    line_copy.start()
    loads = []
    for k in range(groups):
        pair = (
            pltpu.make_async_copy(fwd.at[:, :, k], f_bufs[k], in_sem.at[2 * k]),
            pltpu.make_async_copy(adj.at[:, :, k], a_bufs[k], in_sem.at[2 * k + 1]),
        )
        for copy in pair:
            copy.start()
        loads.append(pair)

    barrier = pltpu.get_barrier_semaphore()

    @pl.loop(1, devices)
    def _(o):
        pl.semaphore_signal(barrier, inc=1, device_id=everyone(o), device_id_type=MESH)

    line_copy.wait()
    re, im = line[0, ms : ms + 1, :], line[1, ms : ms + 1, :]
    m_re, m_im = mode[0:1, :], mode[1:2, :]
    over_re = jnp.sum(re * m_re - im * m_im, axis=1, keepdims=True)
    over_im = jnp.sum(re * m_im + im * m_re, axis=1, keepdims=True)
    fom = jnp.broadcast_to((over_re * over_re + over_im * over_im) / cols, (1, LANES))
    f_src[...] = fom

    pl.semaphore_wait(barrier, devices - 1)

    def share(src, recv, ssem, rsem):
        def copy(o):
            return pltpu.make_async_remote_copy(
                src_ref=src, dst_ref=recv.at[o - 1],
                send_sem=ssem.at[o - 1], recv_sem=rsem.at[o - 1],
                device_id=everyone(o), device_id_type=MESH,
            )

        @pl.loop(1, devices)
        def _(o):
            copy(o).start()

        return copy

    f_copy = share(f_src, f_recv, f_ssem, f_rsem)
    slope[...] = 4.0 * (1.0 - jnp.tanh(4.0 * (density[...] - 0.5)) ** 2)

    def finish(copy):
        @pl.loop(1, devices)
        def _(o):
            copy(o).wait()

    finish(f_copy)
    total_fom = fom + jnp.sum(f_recv[...], axis=0)
    scale = total_fom / devices + 1.0
    weight = target[0] - fom / scale
    freq = 1.0 + wl_index[0].astype(jnp.float32) / devices
    factor = jnp.max(weight) * freq * freq

    def order(piece):
        return (g1, g2) if piece % 2 == 0 else (g2, g1)

    def build(k):
        for copy in loads[k]:
            copy.wait()
        for half in range(cores):

            @pl.loop(0, per_core)
            def _(i):
                oz = i % deep
                hi, lo = (i // deep) // g2, (i // deep) % g2
                c = (c_me + half) % cores
                z = (z_me + oz) % deep
                d = ((((a_me + hi) % g1) * g2 + (b_me + lo) % g2) * cores + c) * deep + z
                t = tile_of[d]
                slot = ((lo * g1) + hi) * deep + oz
                for p in range(parts):
                    cs = slice(p * width, (p + 1) * width)
                    value = factor * (
                        f_bufs[k][0, t, :, cs] * a_bufs[k][0, t, :, cs]
                        - f_bufs[k][1, t, :, cs] * a_bufs[k][1, t, :, cs]
                    )
                    piece = k * parts + p
                    where = i if piece % 2 == 0 else slot
                    if half == 0:
                        own[piece, where] = value
                    else:
                        away[piece, where] = value

    def swap(piece):
        return pltpu.make_async_remote_copy(
            src_ref=away.at[piece], dst_ref=r0.at[piece],
            send_sem=s0.at[piece], recv_sem=e0.at[piece],
            device_id=at(a_me, b_me, (c_me + 1) % cores, z_me), device_id_type=MESH,
        )

    def scatter(piece, step):
        n1, n2 = order(piece)
        n = (n1, n2, deep)[step]
        span = (n2 * deep, deep, 1)[step]
        recv, ssem, rsem = ((r1, s1, e1), (r2, s2, e2), (r3, s3, e3))[step]
        axis = step if step == 2 else (step + piece) % 2
        copies = []
        for o in range(1, n):
            where = (
                at((a_me + o) % g1, b_me, c_me, z_me) if axis == 0
                else at(a_me, (b_me + o) % g2, c_me, z_me) if axis == 1
                else at(a_me, b_me, c_me, (z_me + o) % deep)
            )
            copies.append(pltpu.make_async_remote_copy(
                src_ref=own.at[piece, pl.ds(o * span, span)],
                dst_ref=recv.at[piece, pl.ds((o - 1) * span, span)],
                send_sem=ssem.at[piece, o - 1], recv_sem=rsem.at[piece, o - 1],
                device_id=where, device_id_type=MESH,
            ))
        return copies, recv, span, n

    def start(piece, step):
        for copy in scatter(piece, step)[0]:
            copy.start()

    def add(piece, step):
        copies, recv, span, n = scatter(piece, step)
        for copy in copies:
            copy.wait_recv()

        @pl.loop(0, span)
        def _(i):
            value = own[piece, i]
            for o in range(n - 1):
                value = value + recv[piece, o * span + i]
            own[piece, i] = value

    pieces = groups * parts

    def first(piece):
        if cores > 1:
            swap(piece).wait_recv()

            @pl.loop(0, per_core)
            def _(i):
                own[piece, i] = own[piece, i] + r0[piece, i]

        start(piece, 0)

    built = 0
    for turn in range(pieces // 2 + 3):
        def open_pair(pair):
            nonlocal built
            while built * parts < 2 * pair + 2:
                build(built)
                if cores > 1:
                    for p in range(parts):
                        swap(built * parts + p).start()
                built += 1
            for piece in (2 * pair, 2 * pair + 1):
                first(piece)

        if turn == 0:
            open_pair(0)
            if pieces // 2 > 1:
                open_pair(1)
        if turn < pieces // 2:
            for piece in (2 * turn, 2 * turn + 1):
                add(piece, 0)
                start(piece, 1)
            if turn + 2 < pieces // 2:
                open_pair(turn + 2)
        if 1 <= turn <= pieces // 2:
            for piece in (2 * turn - 2, 2 * turn - 1):
                add(piece, 1)
                start(piece, 2)

    squares = jnp.zeros((1, 1), jnp.float32)
    for piece in range(pieces):
        copies, recv, span, n = scatter(piece, 2)
        for copy in copies:
            copy.wait_recv()
        value = own[piece, 0]
        for o in range(n - 1):
            value = value + recv[piece, o]
        k, p = piece // parts, piece % parts
        rs, cs = slice(k * SUB, (k + 1) * SUB), slice(p * width, (p + 1) * width)
        shaped = value * slope[rs, cs]
        shaped_out[rs, cs] = shaped
        squares = squares + jnp.sum(shaped * shaped, keepdims=True)
    mine = jnp.broadcast_to(squares, (1, LANES))
    q_src[...] = mine
    q_copy = share(q_src, q_recv, q_ssem, q_rsem)

    for piece in range(pieces):
        if cores > 1:
            swap(piece).wait_send()
        for step in range(3):
            for copy in scatter(piece, step)[0]:
                copy.wait_send()
    finish(q_copy)
    squares_out[...] = mine + jnp.sum(q_recv[...], axis=0)


def per_device(forward, adjoint, mode, target, wl_index, tile_of, density):
    wide, deep = lax.axis_size("wl"), lax.axis_size("tile")
    devices = wide * deep
    rows, cols = forward.shape[2:]
    g1, g2, cores = plane(wide)
    tile_rows = rows // devices
    groups = tile_rows // SUB
    parts = max(1, min(PIECES // groups, cols // LANES))
    pieces = groups * parts
    width = cols // parts
    per_core = g1 * g2 * deep
    fwd = forward.reshape(2, devices, groups, SUB, cols)
    adj = adjoint.reshape(2, devices, groups, SUB, cols)
    f32 = jnp.float32
    dma = pltpu.SemaphoreType.DMA
    most = max(g1, g2, 2) - 1
    block = lambda n: pltpu.VMEM((pieces, max(n, 1), SUB, width), f32)
    sizes = (g1, g2, cores, deep, groups, parts, rows, cols)
    peers = max(devices - 1, 1)
    vmem = pl.BlockSpec(memory_space=pltpu.VMEM)
    smem = pl.BlockSpec(memory_space=pltpu.SMEM)
    hbm = pl.BlockSpec(memory_space=pl.ANY)
    third = max(deep - 1, 1)
    shaped, squares = pl.pallas_call(
        functools.partial(kernel, sizes),
        out_shape=(
            jax.ShapeDtypeStruct((tile_rows, cols), f32),
            jax.ShapeDtypeStruct((1, LANES), f32),
        ),
        in_specs=[smem, smem, smem, vmem, vmem, hbm, hbm],
        out_specs=(vmem, vmem),
        scratch_shapes=[
            pltpu.VMEM((2, SUB, cols), f32),
            pltpu.VMEM((1, LANES), f32),
            pltpu.VMEM((peers, 1, LANES), f32),
            pltpu.VMEM((1, LANES), f32),
            pltpu.VMEM((peers, 1, LANES), f32),
            pltpu.VMEM((tile_rows, cols), f32),
            block(per_core),
            block(per_core),
            block(per_core),
            block(per_core),
            block(per_core // min(g1, g2)),
            block(third),
            dma((2 * groups + 1,)),
            dma((peers,)), dma((peers,)), dma((peers,)), dma((peers,)),
            dma((pieces,)), dma((pieces,)),
            dma((pieces, most)), dma((pieces, most)),
            dma((pieces, most)), dma((pieces, most)),
            dma((pieces, third)), dma((pieces, third)),
        ]
        + [pltpu.VMEM((2, devices, SUB, cols), f32)] * (2 * groups),
        compiler_params=pltpu.CompilerParams(
            collective_id=0, has_side_effects=True, vmem_limit_bytes=60 * 2**20
        ),
        name="assemble",
    )(tile_of, target, wl_index, mode, density, fwd, adj)
    return shaped / jnp.sqrt(squares[0, 0] / (rows * cols) + 1e-06)


def solution(mesh):
    in_specs = (
        P(("wl", "tile"), None, None, None),
        P(("wl", "tile"), None, None, None),
        P(),
        P(("wl", "tile")),
        P(("wl", "tile")),
        P(),
        P(("wl", "tile"), None),
    )
    out_specs = P(("wl", "tile"), None)
    return jax.shard_map(
        per_device, mesh=mesh, in_specs=in_specs, out_specs=out_specs, check_vma=False
    )
```

time: 237 us -> 52.4 us (0.22)
  waiting for transfers between devices: 117 us -> 0 us
  blocking collectives: 81.5 us -> 0 us
  Pallas kernels: 0 us -> 48.6 us
  between operations: 18.5 us -> 2.03 us
  other arithmetic: 12.7 us -> 1.58 us
  local copies, waits for them, and re-layouts: 7.4 us -> 0 us
    reduce_scatter x2 -> x0, waiting for transfers between devices: 117 us -> none  [the longest x1 76.9 us: per_device(): lax.psum_scatter((weight * field).reshape(devices, tile_rows, cols)[order...]
    psum x2 -> x0, blocking collectives: 81.5 us -> none  [the longest x1 42 us: per_device(): total_fom = lax.psum(fom, ('wl', 'tile'))]
    pallas_call x0 -> x1, Pallas kernels: none -> 48.6 us  [per_device(): pl.pallas_call(functools.partial(kernel, sizes), out_shape=(jax.ShapeDtyp...]
    mul x1 -> x0, other arithmetic: 8.8 us -> none  [per_device(): weight * field]
    gather x1 -> x0, local copies, waits for them, and re-layouts: 4.93 us -> none  [per_device(): (weight * field).reshape(devices, tile_rows, cols)[order]]
  transfers between devices with their start and end apart: 2 -> 0, of which waited for: 2 -> 0; matrix products, arithmetic and copies ran while one was open for 0% -> 0% of each run, Pallas kernels for 0% -> 0%
where the time goes in v1:
time: 52.4 us; the launch traced here: 52.2 us
  Pallas kernels  48.6 us (93%)
  between operations  2.03 us (4%)
  other arithmetic  1.58 us (3%)
    pallas_call x1, Pallas kernels, per_device(): pl.pallas_call(functools.partial(kernel, sizes), out_shape=(jax.ShapeDtyp...  48.6 us
    div x1, other arithmetic, per_device(): return shaped / jnp.sqrt(squares[0, 0] / (rows * cols) + 1e-06)  1.58 us

profile of v1, /device:TPU:0, one launch (start us, length us, event | category | flops | bytes accessed | tf_op | source)
XLA Modules:
  0.0 52.2 jit_solution(12715561785489768446)
XLA Ops:
  1.3 48.6 %assemble.1 = (f32[32,1024]{1,0:T(8,128)}, f32[1,128]{1,0:T(1,128)}) custom-call(s32[32]{0:T(128)} %tile_of.1, f32[1]{0:T(128)S(6)} %copy.8.target, s32[1]{0:T(128)S(6)} %copy.9.wl_index, f32[2,1024]{1,0:T(2,128)} %mode.1, f32[32,1024]{1,0:T(8,128)} %density.1, f32[2,32,4,8,1024]{4,3,2,1,0:T(8,128)} %bitcast.4, f32[2,32,4,8,1024]{4,3,2,1,0:T(8,128)} %bitcast.5), custom_call_target="tpu_custom_call" | custom-call | tf_op jit(solution)/shard_map/assemble/pallas_call | solution.py:271
  50.6 1.6 %broadcast_divide_fusion = f32[32,1024]{1,0:T(8,128)} fusion(f32[32,1024]{1,0:T(8,128)} %get-tuple-element.7, f32[]{:T(128)} %bitcast.2), kind=kLoop, calls=%fused_computation | loop fusion | flops 32768 | bytes 262148 | tf_op jit(solution)/shard_map/div | solution.py:305

commit v2 on v1

--- a/solution.py
+++ b/solution.py
@@ -10,7 +10,8 @@
 MESH = pl.DeviceIdType.MESH
 SUB = 8
 LANES = 128
-PIECES = 8
+PIECES = 16
+AHEAD = 3
 
 
 def plane(wide):
@@ -21,9 +22,10 @@
 
 
 def kernel(
-    sizes, tile_of, target, wl_index, mode, density, fwd, adj, shaped_out, squares_out,
+    sizes, pair_in, tiles_in, mode_in, density_in, fwd, adj, shaped_hbm, norm_out,
+    own_pair, tile_of, mode, density, shaped_out,
     line, f_src, f_recv, q_src, q_recv, slope, own, away, r0, r1, r2, r3,
-    in_sem, f_ssem, f_rsem, q_ssem, q_rsem, s0, e0, s1, e1, s2, e2, s3, e3, *bufs,
+    in_sem, side_sem, f_ssem, f_rsem, q_ssem, q_rsem, s0, e0, s1, e1, s2, e2, s3, e3, *bufs,
 ):
     g1, g2, cores, deep, groups, parts, rows, cols = sizes
     wide = g1 * g2 * cores
@@ -45,27 +47,34 @@
         f = (me + o) % devices
         return (f // deep, f % deep)
 
+    barrier = pltpu.get_barrier_semaphore()
+
+    @pl.loop(1, devices)
+    def _(o):
+        pl.semaphore_signal(barrier, inc=1, device_id=everyone(o), device_id_type=MESH)
+
     mon = rows // 2
     mt, mk, ms = mon // tile_rows, (mon % tile_rows) // SUB, mon % SUB
     line_copy = pltpu.make_async_copy(fwd.at[:, mt, mk], line, in_sem.at[2 * groups])
-    line_copy.start()
+    mode_copy = pltpu.make_async_copy(mode_in, mode, side_sem.at[0])
+    tile_copy = pltpu.make_async_copy(tiles_in, tile_of, side_sem.at[1])
+    density_copy = pltpu.make_async_copy(density_in, density, side_sem.at[2])
+    pair_copy = pltpu.make_async_copy(pair_in, own_pair, side_sem.at[4])
+    for copy in (line_copy, mode_copy, tile_copy, density_copy, pair_copy):
+        copy.start()
     loads = []
     for k in range(groups):
         pair = (
             pltpu.make_async_copy(fwd.at[:, :, k], f_bufs[k], in_sem.at[2 * k]),
             pltpu.make_async_copy(adj.at[:, :, k], a_bufs[k], in_sem.at[2 * k + 1]),
         )
-        for copy in pair:
-            copy.start()
+        if k == 0:
+            for copy in pair:
+                copy.start()
         loads.append(pair)
 
-    barrier = pltpu.get_barrier_semaphore()
-
-    @pl.loop(1, devices)
-    def _(o):
-        pl.semaphore_signal(barrier, inc=1, device_id=everyone(o), device_id_type=MESH)
-
     line_copy.wait()
+    mode_copy.wait()
     re, im = line[0, ms : ms + 1, :], line[1, ms : ms + 1, :]
     m_re, m_im = mode[0:1, :], mode[1:2, :]
     over_re = jnp.sum(re * m_re - im * m_im, axis=1, keepdims=True)
@@ -90,6 +99,10 @@
         return copy
 
     f_copy = share(f_src, f_recv, f_ssem, f_rsem)
+    for pair in loads[1:]:
+        for copy in pair:
+            copy.start()
+    density_copy.wait()
     slope[...] = 4.0 * (1.0 - jnp.tanh(4.0 * (density[...] - 0.5)) ** 2)
 
     def finish(copy):
@@ -100,9 +113,12 @@
     finish(f_copy)
     total_fom = fom + jnp.sum(f_recv[...], axis=0)
     scale = total_fom / devices + 1.0
-    weight = target[0] - fom / scale
-    freq = 1.0 + wl_index[0].astype(jnp.float32) / devices
-    factor = jnp.max(weight) * freq * freq
+    pair_copy.wait()
+    weight = own_pair[0] - fom / scale
+    freq = 1.0 + own_pair[1] / devices
+    factor = jnp.concatenate([weight * freq * freq] * (width // LANES), axis=1)
+    factor = jnp.broadcast_to(factor, (SUB, width))
+    tile_copy.wait()
 
     def order(piece):
         return (g1, g2) if piece % 2 == 0 else (g2, g1)
@@ -112,27 +128,21 @@
             copy.wait()
         for half in range(cores):
 
-            @pl.loop(0, per_core)
+            @pl.loop(0, g1 * g2)
             def _(i):
-                oz = i % deep
-                hi, lo = (i // deep) // g2, (i // deep) % g2
+                hi, lo = i // g2, i % g2
                 c = (c_me + half) % cores
-                z = (z_me + oz) % deep
-                d = ((((a_me + hi) % g1) * g2 + (b_me + lo) % g2) * cores + c) * deep + z
-                t = tile_of[d]
-                slot = ((lo * g1) + hi) * deep + oz
-                for p in range(parts):
-                    cs = slice(p * width, (p + 1) * width)
-                    value = factor * (
-                        f_bufs[k][0, t, :, cs] * a_bufs[k][0, t, :, cs]
-                        - f_bufs[k][1, t, :, cs] * a_bufs[k][1, t, :, cs]
-                    )
-                    piece = k * parts + p
-                    where = i if piece % 2 == 0 else slot
-                    if half == 0:
-                        own[piece, where] = value
-                    else:
-                        away[piece, where] = value
+                base = ((((a_me + hi) % g1) * g2 + (b_me + lo) % g2) * cores + c) * deep
+                slots = (i * deep, (lo * g1 + hi) * deep)
+                for oz in range(deep):
+                    t = tile_of[base + (z_me + oz) % deep]
+                    for p in range(parts):
+                        cs = slice(p * width, (p + 1) * width)
+                        piece = k * parts + p
+                        (away if half else own)[piece, slots[piece % 2] + oz] = factor * (
+                            f_bufs[k][0, t, :, cs] * a_bufs[k][0, t, :, cs]
+                            - f_bufs[k][1, t, :, cs] * a_bufs[k][1, t, :, cs]
+                        )
 
     def swap(piece):
         return pltpu.make_async_remote_copy(
@@ -171,48 +181,46 @@
         for copy in copies:
             copy.wait_recv()
 
-        @pl.loop(0, span)
-        def _(i):
-            value = own[piece, i]
-            for o in range(n - 1):
-                value = value + recv[piece, o * span + i]
-            own[piece, i] = value
+        value = own[piece, :span]
+        for o in range(n - 1):
+            value = value + recv[piece, o * span : (o + 1) * span]
+        own[piece, :span] = value
 
     pieces = groups * parts
 
     def first(piece):
         if cores > 1:
             swap(piece).wait_recv()
-
-            @pl.loop(0, per_core)
-            def _(i):
-                own[piece, i] = own[piece, i] + r0[piece, i]
+            own[piece] = own[piece] + r0[piece]
 
         start(piece, 0)
 
     built = 0
-    for turn in range(pieces // 2 + 3):
-        def open_pair(pair):
-            nonlocal built
-            while built * parts < 2 * pair + 2:
-                build(built)
-                if cores > 1:
-                    for p in range(parts):
-                        swap(built * parts + p).start()
-                built += 1
-            for piece in (2 * pair, 2 * pair + 1):
-                first(piece)
-
+
+    def make(upto):
+        nonlocal built
+        while built < min(upto, groups):
+            build(built)
+            if cores > 1:
+                for p in range(parts):
+                    swap(built * parts + p).start()
+            built += 1
+
+    def open_pair(pair):
+        make((2 * pair + 1) // parts + 2)
+        for piece in (2 * pair, 2 * pair + 1):
+            first(piece)
+
+    for turn in range(pieces // 2 + 1):
         if turn == 0:
-            open_pair(0)
-            if pieces // 2 > 1:
-                open_pair(1)
+            for pair in range(min(AHEAD, pieces // 2)):
+                open_pair(pair)
         if turn < pieces // 2:
             for piece in (2 * turn, 2 * turn + 1):
                 add(piece, 0)
                 start(piece, 1)
-            if turn + 2 < pieces // 2:
-                open_pair(turn + 2)
+            if turn + AHEAD < pieces // 2:
+                open_pair(turn + AHEAD)
         if 1 <= turn <= pieces // 2:
             for piece in (2 * turn - 2, 2 * turn - 1):
                 add(piece, 1)
@@ -231,6 +239,8 @@
         shaped = value * slope[rs, cs]
         shaped_out[rs, cs] = shaped
         squares = squares + jnp.sum(shaped * shaped, keepdims=True)
+    out_copy = pltpu.make_async_copy(shaped_out, shaped_hbm, side_sem.at[3])
+    out_copy.start()
     mine = jnp.broadcast_to(squares, (1, LANES))
     q_src[...] = mine
     q_copy = share(q_src, q_recv, q_ssem, q_rsem)
@@ -241,8 +251,10 @@
         for step in range(3):
             for copy in scatter(piece, step)[0]:
                 copy.wait_send()
+    out_copy.wait()
     finish(q_copy)
-    squares_out[...] = mine + jnp.sum(q_recv[...], axis=0)
+    squares = mine + jnp.sum(q_recv[...], axis=0)
+    norm_out[...] = jnp.sqrt(squares / (rows * cols) + 1e-06)
 
 
 def per_device(forward, adjoint, mode, target, wl_index, tile_of, density):
@@ -265,18 +277,22 @@
     sizes = (g1, g2, cores, deep, groups, parts, rows, cols)
     peers = max(devices - 1, 1)
     vmem = pl.BlockSpec(memory_space=pltpu.VMEM)
-    smem = pl.BlockSpec(memory_space=pltpu.SMEM)
     hbm = pl.BlockSpec(memory_space=pl.ANY)
     third = max(deep - 1, 1)
-    shaped, squares = pl.pallas_call(
+    shaped, norm = pl.pallas_call(
         functools.partial(kernel, sizes),
         out_shape=(
             jax.ShapeDtypeStruct((tile_rows, cols), f32),
             jax.ShapeDtypeStruct((1, LANES), f32),
         ),
-        in_specs=[smem, smem, smem, vmem, vmem, hbm, hbm],
-        out_specs=(vmem, vmem),
+        in_specs=[hbm, hbm, hbm, hbm, hbm, hbm],
+        out_specs=(hbm, vmem),
         scratch_shapes=[
+            pltpu.SMEM((2,), f32),
+            pltpu.SMEM((devices,), jnp.int32),
+            pltpu.VMEM(mode.shape, f32),
+            pltpu.VMEM((tile_rows, cols), f32),
+            pltpu.VMEM((tile_rows, cols), f32),
             pltpu.VMEM((2, SUB, cols), f32),
             pltpu.VMEM((1, LANES), f32),
             pltpu.VMEM((peers, 1, LANES), f32),
@@ -290,6 +306,7 @@
             block(per_core // min(g1, g2)),
             block(third),
             dma((2 * groups + 1,)),
+            dma((5,)),
             dma((peers,)), dma((peers,)), dma((peers,)), dma((peers,)),
             dma((pieces,)), dma((pieces,)),
             dma((pieces, most)), dma((pieces, most)),
@@ -301,8 +318,8 @@
             collective_id=0, has_side_effects=True, vmem_limit_bytes=60 * 2**20
         ),
         name="assemble",
-    )(tile_of, target, wl_index, mode, density, fwd, adj)
-    return shaped / jnp.sqrt(squares[0, 0] / (rows * cols) + 1e-06)
+    )(jnp.concatenate([target, wl_index.astype(f32)]), tile_of, mode, density, fwd, adj)
+    return shaped / norm[0, 0]
 
 
 def solution(mesh):

time: 52.4 us -> 49.3 us (0.941)
  Pallas kernels: 48.6 us -> 44.9 us
  other arithmetic: 1.58 us -> 2.84 us
  between operations: 2.03 us -> 1.31 us
    pallas_call x1, Pallas kernels: 48.6 us -> 44.9 us  [per_device(): pl.pallas_call(functools.partial(kernel, sizes), out_shape=(jax.ShapeDtyp...]
    div x1, other arithmetic: 1.58 us -> 2.26 us  [per_device(): return shaped / norm[0, 0]]
    concatenate x0 -> x1, other arithmetic: none -> 0.59 us  [per_device(): jnp.concatenate([target, wl_index.astype(f32)])]
where the time goes in v2:
time: 49.3 us; the launch traced here: 49.1 us
  Pallas kernels  44.9 us (91%)
  other arithmetic  2.84 us (6%)
  between operations  1.31 us (3%)
    pallas_call x1, Pallas kernels, per_device(): pl.pallas_call(functools.partial(kernel, sizes), out_shape=(jax.ShapeDtyp...  44.9 us
    div x1, other arithmetic, per_device(): return shaped / norm[0, 0]  2.26 us

profile of v2, /device:TPU:0, one launch (start us, length us, event | category | flops | bytes accessed | tf_op | source)
XLA Modules:
  0.0 49.1 jit_solution(3901775150281568488)
XLA Ops:
  1.3 0.6 %pad_maximum_fusion.pair_in = f32[2]{0:T(128)} fusion(f32[1]{0:T(128)S(6)} %convert_element_type.3, f32[1]{0:T(128)S(6)} %copy.8), kind=kLoop, calls=%fused_computation.1 | loop fusion | flops 2 | bytes 16 | tf_op jit(solution)/shard_map/concatenate | solution.py:321
  1.9 44.9 %assemble.1 = (f32[32,1024]{1,0:T(8,128)}, f32[1,128]{1,0:T(1,128)}) custom-call(f32[2]{0:T(128)} %pad_maximum_fusion.pair_in, s32[32]{0:T(128)} %tiles_in.1, f32[2,1024]{1,0:T(2,128)} %mode_in.1, f32[32,1024]{1,0:T(8,128)} %density_in.1, f32[2,32,4,8,1024]{4,3,2,1,0:T(8,128)} %bitcast.4, f32[2,32,4,8,1024]{4,3,2,1,0:T(8,128)} %bitcast.5), custom_call_target="tpu_custom_call" | custom-call | tf_op jit(solution)/shard_map/assemble/pallas_call | solution.py:282
  46.8 2.3 %broadcast_divide_fusion = f32[32,1024]{1,0:T(8,128)} fusion(f32[32,1024]{1,0:T(8,128)} %get-tuple-element.7, f32[]{:T(128)} %bitcast.6), kind=kLoop, calls=%fused_computation | loop fusion | flops 32768 | bytes 262148 | tf_op jit(solution)/shard_map/div | solution.py:322
